TPU v7x, 32 devices: a whole 2x2x4 slice. The times are simulated.
32 devices in a mesh: cand: 4 (over y, core), tensor: 8 (over z, x).
Axes of the slice: x: 2, y: 2, z: 4, core: 2. Of those that a mesh axis runs over, the one named last changes fastest.
Arguments:
- states: bfloat16 [512, 3584], P('cand'), may hold values from -60 to 60
- targets: int32 [512], replicated, may hold values from 0 to 131071
- loss_mask: int32 [512], P('cand'), may hold values 0 or 1
- cand_of: int32 [4], replicated, may hold values from 0 to 3
- lambdas: float32 [4], replicated, may hold values from 0.2 to 1
- base_q: bfloat16 [3584, 4096], P('cand', 'tensor'), may hold values from -0.09375 to 0.09375
- delta_q: bfloat16 [2, 3584, 4096], P(None, 'cand', 'tensor'), may hold values from -0.046875 to 0.046875
- base_k: bfloat16 [3584, 2048], P('cand'), may hold values from -0.09375 to 0.09375
- delta_k: bfloat16 [2, 3584, 2048], P(None, 'cand'), may hold values from -0.046875 to 0.046875
- base_v: bfloat16 [3584, 2048], P('cand'), may hold values from -0.09375 to 0.09375
- delta_v: bfloat16 [2, 3584, 2048], P(None, 'cand'), may hold values from -0.046875 to 0.046875
- base_o: bfloat16 [4096, 3584], P('tensor', 'cand'), may hold values from -0.09375 to 0.09375
- delta_o: bfloat16 [2, 4096, 3584], P(None, 'tensor', 'cand'), may hold values from -0.046875 to 0.046875
- pre_gain: float32 [3584], replicated, may hold values from 0.5 to 2
- post_gain: float32 [3584], replicated, may hold values from 0.5 to 2
- final_gain: float32 [3584], replicated, may hold values from 0.5 to 2
- unembed: bfloat16 [3584, 131072], P(None, ('cand', 'tensor')), may hold values from -0.3125 to 0.3125
Outputs:
- token_loss: float32 [512], P('cand')
- cand_loss: float32 [4], replicated
All inputs are finite; a program needn't handle non-finite values. No bound on the sum of `loss_mask` on one device may be relied on, other than what follows from the above.
Results may differ from a plain program's by a relative error of at most 0.002.
Values may be sent and summed in bfloat16 or wider, within the bound.
No kernel may reach another device: no remote copies, remote signals or barrier semaphores. Data moves between devices by JAX's collectives and lax.ppermute only.
A program may use at most 128 MiB of HBM per device.

v0:
```python
import math
import jax
import jax.numpy as jnp
from jax import lax
from jax.sharding import PartitionSpec as P

KV = 8
HEAD_SIZE = 256
CANDS = 4


def root_norm(entries, scale_gain):
    mean_square = jnp.mean(entries * entries, axis=-1, keepdims=True)
    return entries * lax.rsqrt(mean_square + 1e-06) * scale_gain


def rotate_pairs(entries, length):
    half_width = entries.shape[-1] // 2
    positions = jnp.arange(length).astype(jnp.float32)
    frequency = jnp.exp(
        -math.log(10000.0) * jnp.arange(half_width).astype(jnp.float32) * 2.0 / entries.shape[-1]
    )
    angles = positions[:, None] * frequency[None, :]
    cosine = jnp.cos(angles)[:, None, :]
    sine_part = jnp.sin(angles)[:, None, :]
    first = entries[..., :half_width]
    second = entries[..., half_width:]
    return jnp.concatenate(
        [first * cosine - second * sine_part, second * cosine + first * sine_part], axis=-1
    )


def task_total(delta):
    return jnp.sum(delta.astype(jnp.float32), axis=0).astype(jnp.bfloat16)


def merge_weights(base, total, mixing):
    return (base.astype(jnp.float32) + mixing * total.astype(jnp.float32)).astype(jnp.bfloat16)


def on_device(
    states,
    targets,
    loss_mask,
    cand_of,
    lambdas,
    base_q,
    delta_q,
    base_k,
    delta_k,
    base_v,
    delta_v,
    base_o,
    delta_o,
    pre_gain,
    post_gain,
    final_gain,
    unembed,
):
    cand_id = lax.axis_index("cand")
    tensor_id = lax.axis_index("tensor")
    tensor_count = lax.axis_size("tensor")
    chosen = cand_of[cand_id]
    mixing = lambdas[chosen]
    group_size = tensor_count // KV
    head_start = tensor_id // group_size * HEAD_SIZE
    own_base_k = lax.dynamic_slice_in_dim(base_k, head_start, HEAD_SIZE, 1)
    own_base_v = lax.dynamic_slice_in_dim(base_v, head_start, HEAD_SIZE, 1)
    own_delta_k = lax.dynamic_slice_in_dim(delta_k, head_start, HEAD_SIZE, 2)
    own_delta_v = lax.dynamic_slice_in_dim(delta_v, head_start, HEAD_SIZE, 2)
    summed = [task_total(delta) for delta in (delta_q, own_delta_k, own_delta_v, delta_o)]
    pieces = (
        lax.all_gather(base_q, "cand", axis=0, tiled=True),
        lax.all_gather(own_base_k, "cand", axis=0, tiled=True),
        lax.all_gather(own_base_v, "cand", axis=0, tiled=True),
        lax.all_gather(base_o, "cand", axis=1, tiled=True),
        lax.all_gather(summed[0], "cand", axis=0, tiled=True),
        lax.all_gather(summed[1], "cand", axis=0, tiled=True),
        lax.all_gather(summed[2], "cand", axis=0, tiled=True),
        lax.all_gather(summed[3], "cand", axis=1, tiled=True),
    )
    base_parts = pieces[:4]
    task_parts = pieces[4:]
    w_query = merge_weights(base_parts[0], task_parts[0], mixing)
    w_key = merge_weights(base_parts[1], task_parts[1], mixing)
    w_value = merge_weights(base_parts[2], task_parts[2], mixing)
    w_out = merge_weights(base_parts[3], task_parts[3], mixing)
    length = states.shape[0]
    stream = states.astype(jnp.float32)
    normed = root_norm(stream, pre_gain).astype(jnp.bfloat16)
    query_rows = jnp.dot(normed, w_query, preferred_element_type=jnp.float32).reshape(
        length, -1, HEAD_SIZE
    )
    query_rows = rotate_pairs(query_rows, length).astype(jnp.bfloat16)
    key_full = jnp.dot(normed, w_key, preferred_element_type=jnp.float32).astype(jnp.bfloat16)
    value_full = jnp.dot(normed, w_value, preferred_element_type=jnp.float32).astype(jnp.bfloat16)
    key_matrix = rotate_pairs(
        key_full.astype(jnp.float32).reshape(length, 1, HEAD_SIZE), length
    ).astype(jnp.bfloat16)[:, 0, :]
    attention_scores = jnp.einsum(
        "lhd,md->hlm", query_rows, key_matrix, preferred_element_type=jnp.float32
    ) * HEAD_SIZE ** (-0.5)
    attention_scores = 50.0 * jnp.tanh(attention_scores / 50.0)
    causal = jnp.arange(length)[:, None] >= jnp.arange(length)[None, :]
    weights = jnp.where(causal[None, :, :], jnp.exp(attention_scores), 0.0)
    attention_probs = (weights / jnp.sum(weights, axis=-1, keepdims=True)).astype(jnp.bfloat16)
    context_rows = jnp.einsum(
        "hlm,md->lhd", attention_probs, value_full, preferred_element_type=jnp.float32
    )
    context_rows = context_rows.astype(jnp.bfloat16).reshape(length, -1)
    partial_value = jnp.dot(context_rows, w_out, preferred_element_type=jnp.float32)
    vocab_width = unembed.shape[1]
    vocab_start = (cand_id * tensor_count + tensor_id) * vocab_width
    vocab_index = jnp.arange(vocab_width)
    attended = lax.psum(partial_value, "tensor")
    final_rows = root_norm(stream + root_norm(attended, post_gain), final_gain).astype(jnp.bfloat16)
    logits = jnp.dot(
        lax.all_gather(final_rows, "cand", axis=0, tiled=True),
        unembed,
        preferred_element_type=jnp.float32,
    )
    capped = 30.0 * jnp.tanh(logits / 30.0)
    totals = jnp.sum(jnp.exp(capped), axis=1)
    local_ids = targets - vocab_start
    matches = local_ids[:, None] == vocab_index[None, :]
    picked = jnp.sum(jnp.where(matches, capped, 0.0), axis=1)
    vocab_sums = jnp.stack([totals, picked], axis=0)
    summed_terms = lax.psum(vocab_sums, ("cand", "tensor"))
    own_terms = lax.dynamic_slice_in_dim(summed_terms, cand_id * length, length, 1)
    mask_values = loss_mask.astype(jnp.float32)
    token_loss = mask_values * (jnp.log(own_terms[0]) - own_terms[1])
    onehot = (chosen == jnp.arange(CANDS)).astype(jnp.float32)
    loss_sums, counts = lax.psum(
        (onehot * jnp.sum(token_loss), onehot * jnp.sum(mask_values)), "cand"
    )
    return (token_loss, loss_sums / jnp.maximum(counts, 1.0))


def solution(mesh):
    in_specs = (
        P("cand", None),
        P(),
        P("cand"),
        P(),
        P(),
        P("cand", "tensor"),
        P(None, "cand", "tensor"),
        P("cand", None),
        P(None, "cand", None),
        P("cand", None),
        P(None, "cand", None),
        P("tensor", "cand"),
        P(None, "tensor", "cand"),
        P(),
        P(),
        P(),
        P(None, ("cand", "tensor")),
    )
    out_specs = (P("cand"), P())
    return jax.shard_map(
        on_device, mesh=mesh, in_specs=in_specs, out_specs=out_specs, check_vma=False
    )
```

profile of v0, /device:TPU:0, one launch (start us, length us, event | category | flops | bytes accessed | tf_op | source)
XLA Modules:
  0.0 451.5 jit_solution(439209231556427896)
XLA Ops:
  7.2 0.0 all-gather.14.cloned.1.call-start
  7.2 1.9 constant_dynamic-slice_fusion.1
  9.2 0.0 all-gather.16.cloned.1.call-start
  9.2 2.3 dynamic-slice_reduce_fusion
  11.6 0.0 all-gather.20.cloned.1.call-start
  11.6 1.6 reduce_sum.123
  13.2 0.0 all-gather.18.cloned.1.call-start
  13.2 0.5 all-gather.18.cloned.1.call-update
  13.8 0.0 all-gather.10.cloned.1.call-start
  13.8 1.8 constant_dynamic-slice_fusion.2
  15.7 0.0 all-gather.12.cloned.1.call-start
  15.7 2.4 dynamic-slice_reduce_fusion.1
  18.2 0.0 all-gather.24.cloned.1.call-start
  18.2 1.5 reduce_sum.125
  19.7 0.0 all-gather.22.cloned.1.call-start
  19.8 0.7 all-gather.22.cloned.1.call-update
  20.6 0.6 dynamic_slice.22
  23.1 0.6 dynamic_slice.23
  23.7 0.3 fusion.4
  24.0 0.3 multiply_cosine_fusion
  24.3 9.1 %all-gather.14.cloned.1.call-done = bf16[3584,256]{1,0:T(8,128)(2,1)} async-done(((bf16[896,256]{1,0:T(8,128)(2,1)}), bf16[3584,256]{1,0:T(8,128)(2,1)}) %all-gather.14.cloned.1.call-update) | async-done | bytes 1835024 | tf_op jit(solution)/shard_map/all_gather | solution.py:74
  33.4 22.7 %all-gather.16.cloned.1.call-done = bf16[3584,256]{1,0:T(8,128)(2,1)} async-done(((bf16[896,256]{1,0:T(8,128)(2,1)}), bf16[3584,256]{1,0:T(8,128)(2,1)}) %all-gather.16.cloned.1.call-update) | async-done | bytes 1835024 | tf_op jit(solution)/shard_map/all_gather | solution.py:78
  56.1 3.6 fusion.20
  59.7 0.3 fusion.37
  60.0 29.2 %all-gather.20.cloned.1.call-done = bf16[3584,512]{1,0:T(8,128)(2,1)} async-done(((bf16[896,512]{1,0:T(8,128)(2,1)}), bf16[3584,512]{1,0:T(8,128)(2,1)}) %all-gather.20.cloned.1.call-update) | async-done | bytes 3670032 | tf_op jit(solution)/shard_map/all_gather | solution.py:77
  89.2 32.9 %all-gather.18.cloned.1.call-done = bf16[3584,512]{1,0:T(8,128)(2,1)} async-done(((bf16[896,512]{1,0:T(8,128)(2,1)}), bf16[3584,512]{1,0:T(8,128)(2,1)}) %all-gather.18.cloned.1.call-update) | async-done | bytes 3670032 | tf_op jit(solution)/shard_map/all_gather | solution.py:73
  122.1 5.2 %fusion = f32[128,512]{1,0:T(8,128)S(1)} fusion(bf16[3584,512]{1,0:T(8,128)(2,1)} %all-gather.20.cloned.1.call-done, bf16[3584,512]{1,0:T(8,128)(2,1)} %all-gather.18.cloned.1.call-done, f32[]{:T(128)} %bitcast.1, bf16[128,3584]{1,0:T(8,128)(2,1)S(1)} %copy-done.1, f32[3584]{0:T(1024)S(1)} %copy-done.8, f32[128]{0:T(128)S(1)} %add_rsqrt_fusion.2), kind=kOutput, calls=%fused_computation.6 | convolution fusion | flops 480772096 | bytes 8534532 | tf_op jit(solution)/shard_map/dot_general | solution.py:91
  127.3 0.2 reshape.177
  127.5 0.1 fusion.53
  127.7 0.2 fusion.15
  127.9 16.7 %all-gather.10.cloned.1.call-done = bf16[3584,256]{1,0:T(8,128)(2,1)} async-done(((bf16[896,256]{1,0:T(8,128)(2,1)}), bf16[3584,256]{1,0:T(8,128)(2,1)}) %all-gather.10.cloned.1.call-update) | async-done | bytes 1835024 | tf_op jit(solution)/shard_map/all_gather | solution.py:75
  144.6 22.5 %all-gather.12.cloned.1.call-done = bf16[3584,256]{1,0:T(8,128)(2,1)} async-done(((bf16[896,256]{1,0:T(8,128)(2,1)}), bf16[3584,256]{1,0:T(8,128)(2,1)}) %all-gather.12.cloned.1.call-update) | async-done | bytes 1835024 | tf_op jit(solution)/shard_map/all_gather | solution.py:79
  167.2 3.9 convolution_convert_fusion
  171.1 29.1 %all-gather.24.cloned.1.call-done = bf16[512,3584]{1,0:T(8,128)(2,1)} async-done(((bf16[512,896]{1,0:T(8,128)(2,1)}), bf16[512,3584]{1,0:T(8,128)(2,1)}) %all-gather.24.cloned.1.call-update) | async-done | bytes 3670032 | tf_op jit(solution)/shard_map/all_gather | solution.py:80
  200.2 33.1 %all-gather.22.cloned.1.call-done = bf16[512,3584]{1,0:T(8,128)(2,1)} async-done(((bf16[512,896]{1,0:T(8,128)(2,1)}), bf16[512,3584]{1,0:T(8,128)(2,1)}) %all-gather.22.cloned.1.call-update) | async-done | bytes 3670032 | tf_op jit(solution)/shard_map/all_gather | solution.py:76
  233.3 6.6 %fusion.1 = f32[128,3584]{1,0:T(8,128)} fusion(bf16[128,512]{0,1:T(8,128)(2,1)S(1)} %bitcast.38, bf16[512,3584]{1,0:T(8,128)(2,1)} %all-gather.24.cloned.1.call-done, bf16[512,3584]{1,0:T(8,128)(2,1)} %all-gather.22.cloned.1.call-done, f32[]{:T(128)} %bitcast.1), kind=kOutput, calls=%fused_computation.7 | convolution fusion | flops 478937088 | bytes 9306116 | tf_op jit(solution)/shard_map/dot_general | solution.py:111
  239.9 0.2 all-gather.26.cloned.1.call-start
  240.2 95.7 %all-reduce.3.cloned.1.call-done = f32[128,3584]{1,0:T(8,128)} async-done(((f32[128,3584]{1,0:T(8,128)}), f32[128,3584]{1,0:T(8,128)}) %all-reduce.3.cloned.1.call-update) | async-done | bytes 1835024 | tf_op jit(solution)/shard_map/psum | solution.py:115
  335.9 1.8 multiply_reduce_fusion.1
  337.8 2.0 multiply_reduce_fusion
  339.8 1.4 multiply_convert_fusion
  341.3 31.1 %all-gather.26.cloned.1.call-done = bf16[512,3584]{1,0:T(8,128)(2,1)} async-done(((bf16[128,3584]{1,0:T(8,128)(2,1)}), bf16[512,3584]{1,0:T(8,128)(2,1)}) %all-gather.26.cloned.1.call-update) | async-done | bytes 3670032 | tf_op jit(solution)/shard_map/all_gather | solution.py:118
  372.4 22.9 %exponential_reduce_fusion = (f32[512]{0:T(512)S(1)}, f32[512]{0:T(512)S(1)}) fusion(s32[512]{0:T(512)S(1)} %broadcast_subtract_fusion, bf16[512,3584]{1,0:T(8,128)(2,1)} %all-gather.26.cloned.1.call-done, bf16[3584,4096]{1,0:T(8,128)(2,1)} %param.33), kind=kOutput, calls=%fused_computation.2 | convolution fusion | flops 15044968448 | bytes 33036288 | tf_op jit(solution)/shard_map/dot_general | solution.py:117
  395.3 39.3 %psum.29 = f32[2,512]{1,0:T(2,128)S(1)} all-reduce(f32[2,512]{1,0:T(2,128)S(1)} %pad_maximum_fusion), channel_id=1, replica_groups=mesh['cand'=4,'tensor'=8] {'cand','tensor'}, use_global_device_ids=true, to_apply=%region_11.12 | all-reduce | flops 1024 | bytes 8192 | tf_op jit(solution)/shard_map/psum | solution.py:128
  434.7 1.1 fusion.52
  435.8 1.8 compare_select_fusion
  437.6 6.5 %all-reduce = (f32[4]{0:T(128)S(1)}, f32[4]{0:T(128)S(1)}) all-reduce(f32[4]{0:T(128)S(1)} %get-tuple-element.18, f32[4]{0:T(128)S(1)} %get-tuple-element.17), channel_id=1, replica_groups=mesh['cand'=4,'tensor'=8] {'cand'}, use_global_device_ids=true, to_apply=%region_13.14 | all-reduce | flops 8 | bytes 64 | tf_op jit(solution)/shard_map/psum | solution.py:133
  444.2 0.5 maximum_divide_fusion
  (41 shorter events, 0.3 us)
Async XLA Ops:
  7.2 4.4 copy-start.2
  7.2 26.2 %all-gather.14.cloned.1.call-start = ((), (), s32[]{:S(2)}) async-start(), calls=%async_computation.2 | async-start | bytes 2293760 | tf_op jit(solution)/shard_map/all_gather | solution.py:74
  9.2 46.9 %all-gather.16.cloned.1.call-start = ((), (), s32[]{:S(2)}) async-start(), calls=%async_computation.3 | async-start | bytes 2293760 | tf_op jit(solution)/shard_map/all_gather | solution.py:78
  11.6 77.6 %all-gather.20.cloned.1.call-start = ((), (), s32[]{:S(2)}) async-start(), calls=%async_computation.5 | async-start | bytes 4587520 | tf_op jit(solution)/shard_map/all_gather | solution.py:77
  13.2 5.0 %copy-start.3 = (bf16[2,512,896]{2,1,0:T(8,128)(2,1)S(1)}, bf16[2,512,896]{2,1,0:T(8,128)(2,1)}, u32[]{:S(2)}) copy-start(bf16[2,512,896]{2,1,0:T(8,128)(2,1)} %param.29) | copy-start | bytes 5505028
  13.2 108.9 %all-gather.18.cloned.1.call-start = ((), (), s32[]{:S(2)}) async-start(), calls=%async_computation.4 | async-start | bytes 4587520 | tf_op jit(solution)/shard_map/all_gather | solution.py:73
  13.8 130.9 %all-gather.10.cloned.1.call-start = ((), (), s32[]{:S(2)}) async-start(), calls=%async_computation | async-start | bytes 2293760 | tf_op jit(solution)/shard_map/all_gather | solution.py:75
  15.6 4.9 %copy-start.9 = (s32[4]{0:T(128)S(1)}, s32[4]{0:T(128)}, u32[]{:S(2)}) copy-start(s32[4]{0:T(128)} %param.20) | copy-start | bytes 52
  15.6 7.4 %copy-start.10 = (f32[4]{0:T(128)S(1)}, f32[4]{0:T(128)}, u32[]{:S(2)}) copy-start(f32[4]{0:T(128)} %param.21) | copy-start | bytes 52
  15.7 8.1 %copy-start.1 = (bf16[128,3584]{1,0:T(8,128)(2,1)S(1)}, bf16[128,3584]{1,0:T(8,128)(2,1)}, u32[]{:S(2)}) copy-start(bf16[128,3584]{1,0:T(8,128)(2,1)} %param.17) | copy-start | bytes 2752516
  15.7 40.4 %copy-start.8 = (f32[3584]{0:T(1024)S(1)}, f32[3584]{0:T(1024)}, u32[]{:S(2)}) copy-start(f32[3584]{0:T(1024)} %param.30) | copy-start | bytes 43012
  15.7 151.5 %all-gather.12.cloned.1.call-start = ((), (), s32[]{:S(2)}) async-start(), calls=%async_computation.1 | async-start | bytes 2293760 | tf_op jit(solution)/shard_map/all_gather | solution.py:79
  18.2 182.1 %all-gather.24.cloned.1.call-start = ((), (), s32[]{:S(2)}) async-start(), calls=%async_computation.7 | async-start | bytes 4587520 | tf_op jit(solution)/shard_map/all_gather | solution.py:80
  19.7 213.6 %all-gather.22.cloned.1.call-start = ((), (), s32[]{:S(2)}) async-start(), calls=%async_computation.6 | async-start | bytes 4587520 | tf_op jit(solution)/shard_map/all_gather | solution.py:76
  20.5 315.4 %all-reduce.3.cloned.1.call-start = ((), (), s32[]{:S(2)}) async-start(), calls=%async_computation.8 | async-start | bytes 3670016 | tf_op jit(solution)/shard_map/psum | solution.py:115
  239.9 97.8 %copy-start.4 = (f32[3584]{0:T(1024)S(1)}, f32[3584]{0:T(1024)}, u32[]{:S(2)}) copy-start(f32[3584]{0:T(1024)} %param.31) | copy-start | bytes 43012
  239.9 99.9 %copy-start.5 = (f32[3584]{0:T(1024)S(1)}, f32[3584]{0:T(1024)}, u32[]{:S(2)}) copy-start(f32[3584]{0:T(1024)} %param.32) | copy-start | bytes 43012
  239.9 132.5 %all-gather.26.cloned.1.call-start = ((), (), s32[]{:S(2)}) async-start(), calls=%async_computation.9 | async-start | bytes 4587520 | tf_op jit(solution)/shard_map/all_gather | solution.py:118
  335.9 3.9 copy-start
  337.8 3.5 copy-start.6
  341.3 93.4 %copy-start.7 = (s32[128]{0:T(128)S(1)}, s32[128]{0:T(128)}, u32[]{:S(2)}) copy-start(s32[128]{0:T(128)} %param.19) | copy-start | bytes 1540
Sparse Core Ops, SparseCore 0:
  9.5 23.8 all-gather.13
  35.0 21.0 all-gather.15
  57.7 31.4 all-gather.19
  90.6 31.4 all-gather.17
  123.5 21.0 all-gather.9
  146.1 21.0 all-gather.11
  168.7 31.4 all-gather.23
  201.8 31.4 all-gather.21
  240.1 95.7 all-reduce.2
  341.4 30.9 all-gather.25
where the time goes:
time: 452 us
  waiting for transfers between devices  324 us (72%)
  blocking collectives  45.9 us (10%)
  matrix products  42.5 us (9%)
  other arithmetic  17.5 us (4%)
  between operations  16.3 us (4%)
  local copies, waits for them, and re-layouts  5.26 us (1%)
    psum x1, waiting for transfers between devices, on_device(): attended = lax.psum(partial_value, 'tensor')  95.7 us
    psum x1, blocking collectives, on_device(): summed_terms = lax.psum(vocab_sums, ('cand', 'tensor'))  39.3 us
    all_gather x1, waiting for transfers between devices, on_device(): lax.all_gather(base_o, 'cand', axis=1, tiled=True)  33.1 us
    all_gather x1, waiting for transfers between devices, on_device(): lax.all_gather(base_q, 'cand', axis=0, tiled=True)  32.9 us
    all_gather x1, waiting for transfers between devices, on_device(): lax.all_gather(final_rows, 'cand', axis=0, tiled=True)  31.1 us
    all_gather x1, waiting for transfers between devices, on_device(): lax.all_gather(summed[0], 'cand', axis=0, tiled=True)  29.2 us
    all_gather x1, waiting for transfers between devices, on_device(): lax.all_gather(summed[3], 'cand', axis=1, tiled=True)  29.1 us
    dot_general x1, matrix products, on_device(): jnp.dot(lax.all_gather(final_rows, 'cand', axis=0, tiled=True), unembed,...  22.9 us
  transfers between devices with their start and end apart: 10, of which 10 were waited for; matrix products, arithmetic and copies ran while one was open for 6% of the time, Pallas kernels for 0%

commit v1 on v0

--- a/solution.py
+++ b/solution.py
@@ -73,7 +73,7 @@
         lax.all_gather(base_q, "cand", axis=0, tiled=True),
         lax.all_gather(own_base_k, "cand", axis=0, tiled=True),
         lax.all_gather(own_base_v, "cand", axis=0, tiled=True),
-        lax.all_gather(base_o, "cand", axis=1, tiled=True),
+        jnp.concatenate(lax.all_gather(base_o, "cand"), axis=1),
         lax.all_gather(summed[0], "cand", axis=0, tiled=True),
         lax.all_gather(summed[1], "cand", axis=0, tiled=True),
         lax.all_gather(summed[2], "cand", axis=0, tiled=True),

time: 452 us -> 453 us (level)
  waiting for transfers between devices: 324 us -> 302 us
  local copies, waits for them, and re-layouts: 5.26 us -> 22 us
  other arithmetic: 17.5 us -> 22.8 us
    all_gather x1, waiting for transfers between devices: 16.7 us -> 0.11 us  [on_device(): lax.all_gather(own_base_v, 'cand', axis=0, tiled=True)]
    convert_element_type x0 -> x2, local copies, waits for them, and re-layouts: none -> 16.6 us  [merge_weights(): base.astype(jnp.float32) + mixing * total.astype(jnp.float32)]
    all_gather x1, waiting for transfers between devices: 33.1 us -> 27.5 us  [on_device(): lax.all_gather(base_o, 'cand')]
    convert_element_type x0 -> x1, other arithmetic: none -> 5.46 us  [merge_weights(): base.astype(jnp.float32) + mixing * total.astype(jnp.float32)]
  transfers between devices with their start and end apart: 10 -> 10, of which waited for: 10 -> 10; matrix products, arithmetic and copies ran while one was open for 6% -> 10% of each run, Pallas kernels for 0% -> 0%
where the time goes in v1:
time: 453 us; the launch traced here: 452 us
  waiting for transfers between devices  302 us (67%)
  blocking collectives  45.9 us (10%)
  matrix products  43.1 us (10%)
  other arithmetic  22.8 us (5%)
  local copies, waits for them, and re-layouts  22 us (5%)
  between operations  16.3 us (4%)
    psum x1, waiting for transfers between devices, on_device(): attended = lax.psum(partial_value, 'tensor')  95.7 us
    psum x1, blocking collectives, on_device(): summed_terms = lax.psum(vocab_sums, ('cand', 'tensor'))  39.3 us
    all_gather x1, waiting for transfers between devices, on_device(): lax.all_gather(base_q, 'cand', axis=0, tiled=True)  32.9 us
    all_gather x1, waiting for transfers between devices, on_device(): lax.all_gather(final_rows, 'cand', axis=0, tiled=True)  31.1 us
    all_gather x1, waiting for transfers between devices, on_device(): lax.all_gather(summed[3], 'cand', axis=1, tiled=True)  29.3 us
    all_gather x1, waiting for transfers between devices, on_device(): lax.all_gather(summed[0], 'cand', axis=0, tiled=True)  29.2 us
    all_gather x1, waiting for transfers between devices, on_device(): lax.all_gather(base_o, 'cand')  27.5 us
    dot_general x1, matrix products, on_device(): jnp.dot(lax.all_gather(final_rows, 'cand', axis=0, tiled=True), unembed,...  22.9 us
  transfers between devices with their start and end apart: 10, of which 10 were waited for; matrix products, arithmetic and copies ran while one was open for 10% of the time, Pallas kernels for 0%

profile of v1, /device:TPU:0, one launch (start us, length us, event | category | flops | bytes accessed | tf_op | source)
XLA Modules:
  0.0 452.3 jit_solution(3293540329479006012)
XLA Ops:
  7.2 2.0 constant_dynamic-slice_fusion.1
  9.3 0.0 all-gather.17.cloned.1.call-start
  9.3 2.3 dynamic-slice_reduce_fusion
  11.6 0.0 all-gather.21.cloned.1.call-start
  11.7 1.5 reduce_sum.123
  13.2 0.5 all-gather.19.cloned.1.call-update
  13.8 0.5 all-gather.27.cloned.1.call-update
  14.4 1.9 constant_dynamic-slice_fusion.2
  16.4 0.0 all-gather.13.cloned.1.call-start
  16.4 2.2 dynamic-slice_reduce_fusion.1
  18.7 0.0 all-gather.23.cloned.1.call-start
  18.7 1.6 reduce_sum.125
  20.3 0.0 all-reduce.3.cloned.1.call-start
  20.4 0.6 dynamic_slice.22
  22.9 0.6 dynamic_slice.23
  23.6 0.3 fusion.4
  23.8 0.3 multiply_cosine_fusion
  24.1 9.3 %all-gather.15.cloned.1.call-done = bf16[3584,256]{1,0:T(8,128)(2,1)} async-done(((bf16[896,256]{1,0:T(8,128)(2,1)}), bf16[3584,256]{1,0:T(8,128)(2,1)}) %all-gather.15.cloned.1.call-update) | async-done | bytes 1835024 | tf_op jit(solution)/shard_map/all_gather | solution.py:74
  33.4 22.7 %all-gather.17.cloned.1.call-done = bf16[3584,256]{1,0:T(8,128)(2,1)} async-done(((bf16[896,256]{1,0:T(8,128)(2,1)}), bf16[3584,256]{1,0:T(8,128)(2,1)}) %all-gather.17.cloned.1.call-update) | async-done | bytes 1835024 | tf_op jit(solution)/shard_map/all_gather | solution.py:78
  56.1 3.6 fusion.20
  59.7 0.3 fusion.37
  60.0 29.2 %all-gather.21.cloned.1.call-done = bf16[3584,512]{1,0:T(8,128)(2,1)} async-done(((bf16[896,512]{1,0:T(8,128)(2,1)}), bf16[3584,512]{1,0:T(8,128)(2,1)}) %all-gather.21.cloned.1.call-update) | async-done | bytes 3670032 | tf_op jit(solution)/shard_map/all_gather | solution.py:77
  89.2 32.9 %all-gather.19.cloned.1.call-done = bf16[3584,512]{1,0:T(8,128)(2,1)} async-done(((bf16[896,512]{1,0:T(8,128)(2,1)}), bf16[3584,512]{1,0:T(8,128)(2,1)}) %all-gather.19.cloned.1.call-update) | async-done | bytes 3670032 | tf_op jit(solution)/shard_map/all_gather | solution.py:73
  122.1 5.2 %fusion = f32[128,512]{1,0:T(8,128)S(1)} fusion(bf16[3584,512]{1,0:T(8,128)(2,1)} %all-gather.21.cloned.1.call-done, bf16[3584,512]{1,0:T(8,128)(2,1)} %all-gather.19.cloned.1.call-done, f32[]{:T(128)} %bitcast.1, bf16[128,3584]{1,0:T(8,128)(2,1)S(1)} %copy-done.1, f32[3584]{0:T(1024)S(1)} %copy-done.8, f32[128]{0:T(128)S(1)} %add_rsqrt_fusion.2), kind=kOutput, calls=%fused_computation.7 | convolution fusion | flops 480772096 | bytes 8534532 | tf_op jit(solution)/shard_map/dot_general | solution.py:91
  127.3 0.2 reshape.181
  127.5 27.5 %all-gather.27.cloned.1.call-done = bf16[2048,896]{1,0:T(8,128)(2,1)} async-done(((bf16[512,896]{1,0:T(8,128)(2,1)}), bf16[2048,896]{1,0:T(8,128)(2,1)}) %all-gather.27.cloned.1.call-update) | async-done | bytes 3670032 | tf_op jit(solution)/shard_map/all_gather | solution.py:76
  155.0 5.5 %convert_bitcast_fusion = f32[512,4,896]{2,0,1:T(8,128)} fusion(bf16[4,512,896]{2,1,0:T(8,128)(2,1)} %bitcast.44), kind=kLoop, calls=%fused_computation.4 | loop fusion | flops 1835008 | bytes 11010048 | tf_op jit(solution)/shard_map/convert_element_type | solution.py:38
  160.5 8.2 %copy.34 = f32[512,4,896]{0,2,1:T(8,128)} copy(f32[512,4,896]{2,0,1:T(8,128)} %convert_bitcast_fusion) | data formatting | bytes 14680064 | tf_op jit(solution)/shard_map/convert_element_type | solution.py:38
  168.7 8.4 %copy.35 = f32[512,3584]{1,0:T(8,128)} copy(f32[512,3584]{0,1:T(8,128)} %bitcast.43) | data formatting | bytes 14680064 | tf_op jit(solution)/shard_map/convert_element_type | solution.py:38
  177.1 0.1 fusion.53
  177.2 0.2 fusion.15
  177.5 0.1 all-gather.11.cloned.1.call-done
  177.6 22.7 %all-gather.13.cloned.1.call-done = bf16[3584,256]{1,0:T(8,128)(2,1)} async-done(((bf16[896,256]{1,0:T(8,128)(2,1)}), bf16[3584,256]{1,0:T(8,128)(2,1)}) %all-gather.13.cloned.1.call-update) | async-done | bytes 1835024 | tf_op jit(solution)/shard_map/all_gather | solution.py:79
  200.3 3.8 convolution_convert_fusion
  204.1 29.3 %all-gather.23.cloned.1.call-done = bf16[512,3584]{1,0:T(8,128)(2,1)} async-done(((bf16[512,896]{1,0:T(8,128)(2,1)}), bf16[512,3584]{1,0:T(8,128)(2,1)}) %all-gather.23.cloned.1.call-update) | async-done | bytes 3670032 | tf_op jit(solution)/shard_map/all_gather | solution.py:80
  233.4 7.3 %fusion.1 = f32[128,3584]{1,0:T(8,128)} fusion(bf16[128,512]{0,1:T(8,128)(2,1)S(1)} %bitcast.45, f32[512,3584]{1,0:T(8,128)} %copy.35, bf16[512,3584]{1,0:T(8,128)(2,1)} %all-gather.23.cloned.1.call-done, f32[]{:T(128)} %bitcast.1), kind=kOutput, calls=%fused_computation.8 | convolution fusion | flops 477102080 | bytes 12976132 | tf_op jit(solution)/shard_map/dot_general | solution.py:111
  240.7 0.2 all-gather.25.cloned.1.call-start
  241.0 95.7 %all-reduce.3.cloned.1.call-done = f32[128,3584]{1,0:T(8,128)} async-done(((f32[128,3584]{1,0:T(8,128)}), f32[128,3584]{1,0:T(8,128)}) %all-reduce.3.cloned.1.call-update) | async-done | bytes 1835024 | tf_op jit(solution)/shard_map/psum | solution.py:115
  336.7 1.8 multiply_reduce_fusion.1
  338.6 2.0 multiply_reduce_fusion
  340.6 1.4 multiply_convert_fusion
  342.1 31.1 %all-gather.25.cloned.1.call-done = bf16[512,3584]{1,0:T(8,128)(2,1)} async-done(((bf16[128,3584]{1,0:T(8,128)(2,1)}), bf16[512,3584]{1,0:T(8,128)(2,1)}) %all-gather.25.cloned.1.call-update) | async-done | bytes 3670032 | tf_op jit(solution)/shard_map/all_gather | solution.py:118
  373.2 22.9 %exponential_reduce_fusion = (f32[512]{0:T(512)S(1)}, f32[512]{0:T(512)S(1)}) fusion(s32[512]{0:T(512)S(1)} %broadcast_subtract_fusion, bf16[512,3584]{1,0:T(8,128)(2,1)} %all-gather.25.cloned.1.call-done, bf16[3584,4096]{1,0:T(8,128)(2,1)} %param.33), kind=kOutput, calls=%fused_computation.2 | convolution fusion | flops 15044968448 | bytes 33036288 | tf_op jit(solution)/shard_map/dot_general | solution.py:117
  396.1 39.3 %psum.29 = f32[2,512]{1,0:T(2,128)S(1)} all-reduce(f32[2,512]{1,0:T(2,128)S(1)} %pad_maximum_fusion), channel_id=1, replica_groups=mesh['cand'=4,'tensor'=8] {'cand','tensor'}, use_global_device_ids=true, to_apply=%region_11.12 | all-reduce | flops 1024 | bytes 8192 | tf_op jit(solution)/shard_map/psum | solution.py:128
  435.5 1.1 fusion.52
  436.6 1.8 compare_select_fusion
  438.4 6.5 %all-reduce = (f32[4]{0:T(128)S(1)}, f32[4]{0:T(128)S(1)}) all-reduce(f32[4]{0:T(128)S(1)} %get-tuple-element.18, f32[4]{0:T(128)S(1)} %get-tuple-element.17), channel_id=1, replica_groups=mesh['cand'=4,'tensor'=8] {'cand'}, use_global_device_ids=true, to_apply=%region_13.14 | all-reduce | flops 8 | bytes 64 | tf_op jit(solution)/shard_map/psum | solution.py:133
  445.0 0.5 maximum_divide_fusion
  (44 shorter events, 0.5 us)
Async XLA Ops:
  7.2 4.5 copy-start.2
  7.2 26.2 %all-gather.15.cloned.1.call-start = ((), (), s32[]{:S(2)}) async-start(), calls=%async_computation.2 | async-start | bytes 2293760 | tf_op jit(solution)/shard_map/all_gather | solution.py:74
  9.3 46.8 %all-gather.17.cloned.1.call-start = ((), (), s32[]{:S(2)}) async-start(), calls=%async_computation.3 | async-start | bytes 2293760 | tf_op jit(solution)/shard_map/all_gather | solution.py:78
  11.6 77.6 %all-gather.21.cloned.1.call-start = ((), (), s32[]{:S(2)}) async-start(), calls=%async_computation.5 | async-start | bytes 4587520 | tf_op jit(solution)/shard_map/all_gather | solution.py:77
  13.2 5.6 %copy-start.3 = (bf16[2,512,896]{2,1,0:T(8,128)(2,1)S(1)}, bf16[2,512,896]{2,1,0:T(8,128)(2,1)}, u32[]{:S(2)}) copy-start(bf16[2,512,896]{2,1,0:T(8,128)(2,1)} %param.29) | copy-start | bytes 5505028
  13.2 108.9 %all-gather.19.cloned.1.call-start = ((), (), s32[]{:S(2)}) async-start(), calls=%async_computation.4 | async-start | bytes 4587520 | tf_op jit(solution)/shard_map/all_gather | solution.py:73
  13.8 141.2 %all-gather.27.cloned.1.call-start = ((), (), s32[]{:S(2)}) async-start(), calls=%async_computation.9 | async-start | bytes 4587520 | tf_op jit(solution)/shard_map/all_gather | solution.py:76
  14.4 6.0 %copy-start.9 = (s32[4]{0:T(128)S(1)}, s32[4]{0:T(128)}, u32[]{:S(2)}) copy-start(s32[4]{0:T(128)} %param.20) | copy-start | bytes 52
  14.4 8.5 %copy-start.10 = (f32[4]{0:T(128)S(1)}, f32[4]{0:T(128)}, u32[]{:S(2)}) copy-start(f32[4]{0:T(128)} %param.21) | copy-start | bytes 52
  14.4 9.2 %copy-start.1 = (bf16[128,3584]{1,0:T(8,128)(2,1)S(1)}, bf16[128,3584]{1,0:T(8,128)(2,1)}, u32[]{:S(2)}) copy-start(bf16[128,3584]{1,0:T(8,128)(2,1)} %param.17) | copy-start | bytes 2752516
  14.4 163.2 %all-gather.11.cloned.1.call-start = ((), (), s32[]{:S(2)}) async-start(), calls=%async_computation | async-start | bytes 2293760 | tf_op jit(solution)/shard_map/all_gather | solution.py:75
  16.3 39.7 %copy-start.8 = (f32[3584]{0:T(1024)S(1)}, f32[3584]{0:T(1024)}, u32[]{:S(2)}) copy-start(f32[3584]{0:T(1024)} %param.30) | copy-start | bytes 43012
  16.4 183.9 %all-gather.13.cloned.1.call-start = ((), (), s32[]{:S(2)}) async-start(), calls=%async_computation.1 | async-start | bytes 2293760 | tf_op jit(solution)/shard_map/all_gather | solution.py:79
  18.7 214.7 %all-gather.23.cloned.1.call-start = ((), (), s32[]{:S(2)}) async-start(), calls=%async_computation.6 | async-start | bytes 4587520 | tf_op jit(solution)/shard_map/all_gather | solution.py:80
  20.3 316.4 %all-reduce.3.cloned.1.call-start = ((), (), s32[]{:S(2)}) async-start(), calls=%async_computation.7 | async-start | bytes 3670016 | tf_op jit(solution)/shard_map/psum | solution.py:115
  240.7 97.9 %copy-start.4 = (f32[3584]{0:T(1024)S(1)}, f32[3584]{0:T(1024)}, u32[]{:S(2)}) copy-start(f32[3584]{0:T(1024)} %param.31) | copy-start | bytes 43012
  240.7 99.9 %copy-start.5 = (f32[3584]{0:T(1024)S(1)}, f32[3584]{0:T(1024)}, u32[]{:S(2)}) copy-start(f32[3584]{0:T(1024)} %param.32) | copy-start | bytes 43012
  240.7 132.5 %all-gather.25.cloned.1.call-start = ((), (), s32[]{:S(2)}) async-start(), calls=%async_computation.8 | async-start | bytes 4587520 | tf_op jit(solution)/shard_map/all_gather | solution.py:118
  336.7 3.9 copy-start
  338.6 3.5 copy-start.6
  342.1 93.4 %copy-start.7 = (s32[128]{0:T(128)S(1)}, s32[128]{0:T(128)}, u32[]{:S(2)}) copy-start(s32[128]{0:T(128)} %param.19) | copy-start | bytes 1540
Sparse Core Ops, SparseCore 0:
  9.5 23.8 all-gather.14
  35.0 21.0 all-gather.16
  57.7 31.4 all-gather.20
  90.6 31.4 all-gather.18
  123.5 31.4 all-gather.26
  156.4 21.0 all-gather.10
  179.1 21.1 all-gather.12
  201.9 31.4 all-gather.22
  240.8 95.7 all-reduce.2
  342.2 30.9 all-gather.24
